TPU v7x, 256 devices: a whole 4x4x8 slice. The times are simulated.
256 devices in a mesh: row: 4 (over x_lo, core), col: 64 (over y, z, x_hi).
Axes of the slice: x: 4 (x_hi: 2, x_lo: 2; x = x_hi * 2 + x_lo), y: 4, z: 8, core: 2. Of those that a mesh axis runs over, the one named last changes fastest.
Arguments:
- old_table: float32 [64, 4096, 128], P('col', 'row'), may hold values from -1 to 1
- old_blocks: int32 [64, 32], P('col', 'row'), may hold values from 0 to 31, as said below
- new_blocks: int32 [64, 32], P('col', 'row'), may hold values from 0 to 31, as said below
- bag_row_index: int32 [4096, 64, 64], P(None, 'col'), may hold values from 0 to 4095
- bag_length: int32 [4096, 64], P(None, 'col'), may hold values from 1 to 64
- dense: bfloat16 [4096, 128], P(('row', 'col')), may hold values from -6 to 6
- w_first: bfloat16 [2208, 1024], replicated, may hold values from -0.25 to 0.25
- w_second: bfloat16 [1024, 1024], replicated, may hold values from -0.25 to 0.25
- w_out: bfloat16 [1024], replicated, may hold values from -0.75 to 0.75
Outputs:
- logits: float32 [4096], P(('row', 'col'))
- new_tables: float32 [64, 4096, 128], P('col', 'row')
Inputs may be any that keep to these rules, and one draw needn't show every extreme that they name: `old_blocks`: for each table a permutation of the blocks; row device r holds positions r * 8 to (r + 1) * 8 - 1. For each table a permutation of the blocks; for every ordered pair of row devices, exactly 2 of the blocks that the first holds in old_blocks lie on the second in new_blocks.
All inputs are finite; a program needn't handle non-finite values.
Results may differ from a plain program's by a relative error of at most 0.0069.
Values sent between devices are 32-bit elements; how exact they have to be, the bound alone decides.
No kernel may reach another device: no remote copies, remote signals or barrier semaphores. Data moves between devices by JAX's collectives and lax.ppermute only.
A program may use at most 64 MiB of HBM per device.

v0:
```python
import math

import jax
import jax.numpy as jnp
import numpy as np
from jax import lax
from jax.sharding import PartitionSpec as P

BLK = 128


strict_precision = lax.Precision.HIGHEST


def gather_turned(arrays, axis, dims):
    turned = [jnp.moveaxis(a, dim, 0) for a, dim in zip(arrays, dims)]
    widths = [t[0].size for t in turned]
    both = jnp.concatenate([t.reshape(-1, w) for t, w in zip(turned, widths)], axis=1)
    filled = lax.all_gather(both, axis, axis=0, tiled=True)
    tiles = jnp.split(filled, [sum(widths[:k]) for k in range(1, len(widths))], axis=1)
    return tuple(
        (
            jnp.moveaxis(b.reshape(-1, *t.shape[1:]), 0, dim)
            for b, t, dim in zip(tiles, turned, dims)
        )
    )


def in_blocks(x, dim, count):
    before, after = (x.shape[:dim], x.shape[dim + 1 :])
    return jnp.moveaxis(x.reshape(*before, count, -1, *after), dim, 0)


def sent_and_summed(x, axis, dim):
    tiles = in_blocks(x, dim, lax.axis_size(axis))
    arrived = lax.all_to_all(tiles, axis, split_axis=0, concat_axis=0, tiled=True)
    return arrived.sum(axis=0)


def pool_group(bag_rows, block_ids, table_rows):
    block_of = bag_rows // BLK
    matched = block_of[:, :, None] == block_ids[None, None, :]
    slot_order = jnp.arange(block_ids.shape[0], dtype=jnp.int32)
    slot_index = jnp.sum(jnp.where(matched, slot_order[None, None, :], 0), axis=2)
    is_held = jnp.any(matched, axis=2)
    rows_here = jnp.where(is_held, slot_index * BLK + bag_rows % BLK, -1)
    local_order = jnp.arange(table_rows.shape[0], dtype=jnp.int32)
    counts = jnp.sum(
        (rows_here[:, :, None] == local_order[None, None, :]).astype(jnp.float32), axis=1
    )
    return jnp.dot(
        counts, table_rows, precision=strict_precision, preferred_element_type=jnp.float32
    )


def pool_range(wanted, row_count, block_ids, table_rows):
    target_rows = max(8, 8388608 // (wanted.shape[1] * table_rows.shape[0]))
    block_rows = math.gcd(target_rows, row_count)
    grouped_rows = wanted.reshape(row_count // block_rows, block_rows, wanted.shape[1])
    pooled_blocks = lax.map(
        lambda bag_rows: pool_group(bag_rows, block_ids, table_rows), grouped_rows
    )
    return pooled_blocks.reshape(row_count, table_rows.shape[1])


def shards(
    old_table, old_blocks, new_blocks, bag_row_index, bag_length, dense, w_first, w_second, w_out
):
    slot_count = old_blocks.shape[1]
    embedding_width = old_table.shape[2]
    row_devices = lax.axis_size("row")
    my_index = lax.axis_index("row")
    per_peer = slot_count // row_devices
    resident_ids = old_blocks[0]
    target_ids = new_blocks[0]
    resident_rows = old_table[0].reshape(slot_count, BLK, embedding_width)
    all_old, all_new = gather_turned((resident_ids, target_ids), "row", (0, 0))
    positions = jnp.arange(all_old.shape[0], dtype=jnp.int32)
    matches = all_new[:, None] == all_old[None, :]
    source = jnp.sum(jnp.where(matches, positions[None, :], 0), axis=1)
    sender = (source // slot_count).reshape(row_devices, slot_count)
    sender_slot = (source % slot_count).reshape(row_devices, slot_count)
    is_mine = sender == my_index
    rank_order = jnp.cumsum(is_mine.astype(jnp.int32), axis=1) - 1
    rank_values = jnp.arange(per_peer, dtype=jnp.int32)
    chosen = is_mine[:, :, None] & (rank_order[:, :, None] == rank_values[None, None, :])
    outgoing_slots = jnp.sum(jnp.where(chosen, sender_slot[:, :, None], 0), axis=1)
    outgoing = jnp.take(resident_rows, outgoing_slots.reshape(-1), axis=0).reshape(
        row_devices, per_peer, BLK, embedding_width
    )
    arrived = lax.all_to_all(outgoing, "row", split_axis=0, concat_axis=0, tiled=True)
    own_senders = jnp.take(sender, my_index, axis=0)
    sender_hot = (own_senders[:, None] == jnp.arange(row_devices, dtype=jnp.int32)[None, :]).astype(
        jnp.int32
    )
    arrival_rank = jnp.sum(sender_hot * (jnp.cumsum(sender_hot, axis=0) - 1), axis=1)
    moved_rows = jnp.take(
        arrived.reshape(row_devices * per_peer, BLK, embedding_width),
        own_senders * per_peer + arrival_rank,
        axis=0,
    )
    new_tables = moved_rows.reshape(1, slot_count * BLK, embedding_width)
    is_live = jnp.arange(bag_row_index.shape[2], dtype=jnp.int32)[None, :] < bag_length
    wanted = jnp.where(is_live, bag_row_index[:, 0, :], -1)
    share_rows = wanted.shape[0] // row_devices
    table_rows = moved_rows.reshape(slot_count * BLK, embedding_width)
    summed = sent_and_summed(
        pool_range(wanted, share_rows * lax.axis_size("row"), target_ids, table_rows), "row", 0
    )
    pooled = lax.all_to_all(summed[:, None, :], "col", split_axis=0, concat_axis=1, tiled=True)
    dense_wide = dense.astype(jnp.float32)
    stacked_vectors = jnp.concatenate([dense_wide[:, None, :], pooled], axis=1)
    interaction_matrix = jnp.einsum(
        "cxp,cfp->cxf", stacked_vectors, stacked_vectors, precision=strict_precision
    ) * embedding_width ** (-0.5)
    upper_index, lower_index = np.triu_indices(stacked_vectors.shape[1], 1)
    crossed = interaction_matrix[:, upper_index, lower_index]
    joined = jnp.concatenate([dense_wide, crossed], axis=1).astype(jnp.bfloat16)
    hidden_one = jnp.maximum(
        jnp.dot(joined, w_first, preferred_element_type=jnp.float32), 0.0
    ).astype(jnp.bfloat16)
    hidden_two = jnp.maximum(
        jnp.dot(hidden_one, w_second, preferred_element_type=jnp.float32), 0.0
    ).astype(jnp.bfloat16)
    logits = jnp.dot(hidden_two, w_out, preferred_element_type=jnp.float32)
    return (logits, new_tables)


def solution(mesh):
    in_specs = (
        P("col", "row", None),
        P("col", "row"),
        P("col", "row"),
        P(None, "col", None),
        P(None, "col"),
        P(("row", "col"), None),
        P(),
        P(),
        P(),
    )
    out_specs = (P(("row", "col")), P("col", "row", None))
    return jax.shard_map(shards, mesh=mesh, in_specs=in_specs, out_specs=out_specs, check_vma=False)
```

profile of v0, /device:TPU:8, one launch (start us, length us, event | category | flops | bytes accessed | tf_op | source)
XLA Modules:
  0.0 387.0 jit_solution(18126465269378394066)
XLA Ops:
  16.3 5.9 %all-to-all-done = f32[4,2,128,128]{3,2,1,0:T(8,128)S(1)} async-done(((f32[4,2,128,128]{3,2,1,0:T(8,128)}), f32[4,2,128,128]{3,2,1,0:T(8,128)S(1)}, u32[]{:S(2)}, u32[]{:S(2)}) %all-to-all-start) | async-done | bytes 524320 | tf_op jit(solution)/shard_map/all_to_all | solution.py:91
  23.0 264.5 %while.13 = (s32[]{:T(128)}, f32[32,128,128]{2,1,0:T(8,128)}, s32[32,128,64]{1,0,2:T(8,128)}, s32[1,8]{1,0:T(1,128)S(1)}, f32[1024,128]{1,0:T(8,128)S(1)}, /*index=5*/s32[]{:T(128)}) while((s32[]{:T(128)}, f32[32,128,128]{2,1,0:T(8,128)}, s32[32,128,64]{1,0,2:T(8,128)}, s32[1,8]{1,0:T(1,128)S(1)}, f32[1024,128]{1,0:T(8,128)S(1)}, ...), condition=%wide.region_9.11_spmd, body=%wide.region_5.10_spmd.sunk | while | flops 226910208 | bytes 2081417 | solution.py:60
  24.4 5.5 %convert_reduce_fusion.2 = f32[128,1024]{1,0:T(8,128)S(1)} fusion(s32[128,64]{1,0:T(8,128)S(1)} %copy.48), kind=kLoop, calls=%fused_computation.3.clone.1 | loop fusion | flops 25034752 | bytes 557056 | tf_op jit(solution)/shard_map/while/body/eval_jaxpr/reduce_sum | solution.py:48
  32.7 5.5 %convert_reduce_fusion.2 = f32[128,1024]{1,0:T(8,128)S(1)} fusion(s32[128,64]{1,0:T(8,128)S(1)} %copy.48), kind=kLoop, calls=%fused_computation.3.clone.1 | loop fusion | flops 25034752 | bytes 557056 | tf_op jit(solution)/shard_map/while/body/eval_jaxpr/reduce_sum | solution.py:48
  41.0 5.5 %convert_reduce_fusion.2 = f32[128,1024]{1,0:T(8,128)S(1)} fusion(s32[128,64]{1,0:T(8,128)S(1)} %copy.48), kind=kLoop, calls=%fused_computation.3.clone.1 | loop fusion | flops 25034752 | bytes 557056 | tf_op jit(solution)/shard_map/while/body/eval_jaxpr/reduce_sum | solution.py:48
  49.2 5.5 %convert_reduce_fusion.2 = f32[128,1024]{1,0:T(8,128)S(1)} fusion(s32[128,64]{1,0:T(8,128)S(1)} %copy.48), kind=kLoop, calls=%fused_computation.3.clone.1 | loop fusion | flops 25034752 | bytes 557056 | tf_op jit(solution)/shard_map/while/body/eval_jaxpr/reduce_sum | solution.py:48
  57.5 5.5 %convert_reduce_fusion.2 = f32[128,1024]{1,0:T(8,128)S(1)} fusion(s32[128,64]{1,0:T(8,128)S(1)} %copy.48), kind=kLoop, calls=%fused_computation.3.clone.1 | loop fusion | flops 25034752 | bytes 557056 | tf_op jit(solution)/shard_map/while/body/eval_jaxpr/reduce_sum | solution.py:48
  65.8 5.5 %convert_reduce_fusion.2 = f32[128,1024]{1,0:T(8,128)S(1)} fusion(s32[128,64]{1,0:T(8,128)S(1)} %copy.48), kind=kLoop, calls=%fused_computation.3.clone.1 | loop fusion | flops 25034752 | bytes 557056 | tf_op jit(solution)/shard_map/while/body/eval_jaxpr/reduce_sum | solution.py:48
  74.0 5.5 %convert_reduce_fusion.2 = f32[128,1024]{1,0:T(8,128)S(1)} fusion(s32[128,64]{1,0:T(8,128)S(1)} %copy.48), kind=kLoop, calls=%fused_computation.3.clone.1 | loop fusion | flops 25034752 | bytes 557056 | tf_op jit(solution)/shard_map/while/body/eval_jaxpr/reduce_sum | solution.py:48
  82.3 5.5 %convert_reduce_fusion.2 = f32[128,1024]{1,0:T(8,128)S(1)} fusion(s32[128,64]{1,0:T(8,128)S(1)} %copy.48), kind=kLoop, calls=%fused_computation.3.clone.1 | loop fusion | flops 25034752 | bytes 557056 | tf_op jit(solution)/shard_map/while/body/eval_jaxpr/reduce_sum | solution.py:48
  90.6 5.5 %convert_reduce_fusion.2 = f32[128,1024]{1,0:T(8,128)S(1)} fusion(s32[128,64]{1,0:T(8,128)S(1)} %copy.48), kind=kLoop, calls=%fused_computation.3.clone.1 | loop fusion | flops 25034752 | bytes 557056 | tf_op jit(solution)/shard_map/while/body/eval_jaxpr/reduce_sum | solution.py:48
  98.8 5.5 %convert_reduce_fusion.2 = f32[128,1024]{1,0:T(8,128)S(1)} fusion(s32[128,64]{1,0:T(8,128)S(1)} %copy.48), kind=kLoop, calls=%fused_computation.3.clone.1 | loop fusion | flops 25034752 | bytes 557056 | tf_op jit(solution)/shard_map/while/body/eval_jaxpr/reduce_sum | solution.py:48
  115.4 5.5 %convert_reduce_fusion.2 = f32[128,1024]{1,0:T(8,128)S(1)} fusion(s32[128,64]{1,0:T(8,128)S(1)} %copy.48), kind=kLoop, calls=%fused_computation.3.clone.1 | loop fusion | flops 25034752 | bytes 557056 | tf_op jit(solution)/shard_map/while/body/eval_jaxpr/reduce_sum | solution.py:48
  123.6 5.5 %convert_reduce_fusion.2 = f32[128,1024]{1,0:T(8,128)S(1)} fusion(s32[128,64]{1,0:T(8,128)S(1)} %copy.48), kind=kLoop, calls=%fused_computation.3.clone.1 | loop fusion | flops 25034752 | bytes 557056 | tf_op jit(solution)/shard_map/while/body/eval_jaxpr/reduce_sum | solution.py:48
  131.9 5.5 %convert_reduce_fusion.2 = f32[128,1024]{1,0:T(8,128)S(1)} fusion(s32[128,64]{1,0:T(8,128)S(1)} %copy.48), kind=kLoop, calls=%fused_computation.3.clone.1 | loop fusion | flops 25034752 | bytes 557056 | tf_op jit(solution)/shard_map/while/body/eval_jaxpr/reduce_sum | solution.py:48
  140.1 5.5 %convert_reduce_fusion.2 = f32[128,1024]{1,0:T(8,128)S(1)} fusion(s32[128,64]{1,0:T(8,128)S(1)} %copy.48), kind=kLoop, calls=%fused_computation.3.clone.1 | loop fusion | flops 25034752 | bytes 557056 | tf_op jit(solution)/shard_map/while/body/eval_jaxpr/reduce_sum | solution.py:48
  148.4 5.5 %convert_reduce_fusion.2 = f32[128,1024]{1,0:T(8,128)S(1)} fusion(s32[128,64]{1,0:T(8,128)S(1)} %copy.48), kind=kLoop, calls=%fused_computation.3.clone.1 | loop fusion | flops 25034752 | bytes 557056 | tf_op jit(solution)/shard_map/while/body/eval_jaxpr/reduce_sum | solution.py:48
  165.0 5.5 %convert_reduce_fusion.2 = f32[128,1024]{1,0:T(8,128)S(1)} fusion(s32[128,64]{1,0:T(8,128)S(1)} %copy.48), kind=kLoop, calls=%fused_computation.3.clone.1 | loop fusion | flops 25034752 | bytes 557056 | tf_op jit(solution)/shard_map/while/body/eval_jaxpr/reduce_sum | solution.py:48
  173.2 5.5 %convert_reduce_fusion.2 = f32[128,1024]{1,0:T(8,128)S(1)} fusion(s32[128,64]{1,0:T(8,128)S(1)} %copy.48), kind=kLoop, calls=%fused_computation.3.clone.1 | loop fusion | flops 25034752 | bytes 557056 | tf_op jit(solution)/shard_map/while/body/eval_jaxpr/reduce_sum | solution.py:48
  206.3 5.5 %convert_reduce_fusion.2 = f32[128,1024]{1,0:T(8,128)S(1)} fusion(s32[128,64]{1,0:T(8,128)S(1)} %copy.48), kind=kLoop, calls=%fused_computation.3.clone.1 | loop fusion | flops 25034752 | bytes 557056 | tf_op jit(solution)/shard_map/while/body/eval_jaxpr/reduce_sum | solution.py:48
  214.5 5.5 %convert_reduce_fusion.2 = f32[128,1024]{1,0:T(8,128)S(1)} fusion(s32[128,64]{1,0:T(8,128)S(1)} %copy.48), kind=kLoop, calls=%fused_computation.3.clone.1 | loop fusion | flops 25034752 | bytes 557056 | tf_op jit(solution)/shard_map/while/body/eval_jaxpr/reduce_sum | solution.py:48
  222.8 5.5 %convert_reduce_fusion.2 = f32[128,1024]{1,0:T(8,128)S(1)} fusion(s32[128,64]{1,0:T(8,128)S(1)} %copy.48), kind=kLoop, calls=%fused_computation.3.clone.1 | loop fusion | flops 25034752 | bytes 557056 | tf_op jit(solution)/shard_map/while/body/eval_jaxpr/reduce_sum | solution.py:48
  231.1 5.5 %convert_reduce_fusion.2 = f32[128,1024]{1,0:T(8,128)S(1)} fusion(s32[128,64]{1,0:T(8,128)S(1)} %copy.48), kind=kLoop, calls=%fused_computation.3.clone.1 | loop fusion | flops 25034752 | bytes 557056 | tf_op jit(solution)/shard_map/while/body/eval_jaxpr/reduce_sum | solution.py:48
  239.3 5.5 %convert_reduce_fusion.2 = f32[128,1024]{1,0:T(8,128)S(1)} fusion(s32[128,64]{1,0:T(8,128)S(1)} %copy.48), kind=kLoop, calls=%fused_computation.3.clone.1 | loop fusion | flops 25034752 | bytes 557056 | tf_op jit(solution)/shard_map/while/body/eval_jaxpr/reduce_sum | solution.py:48
  247.6 5.5 %convert_reduce_fusion.2 = f32[128,1024]{1,0:T(8,128)S(1)} fusion(s32[128,64]{1,0:T(8,128)S(1)} %copy.48), kind=kLoop, calls=%fused_computation.3.clone.1 | loop fusion | flops 25034752 | bytes 557056 | tf_op jit(solution)/shard_map/while/body/eval_jaxpr/reduce_sum | solution.py:48
  264.1 5.5 %convert_reduce_fusion.2 = f32[128,1024]{1,0:T(8,128)S(1)} fusion(s32[128,64]{1,0:T(8,128)S(1)} %copy.48), kind=kLoop, calls=%fused_computation.3.clone.1 | loop fusion | flops 25034752 | bytes 557056 | tf_op jit(solution)/shard_map/while/body/eval_jaxpr/reduce_sum | solution.py:48
  272.4 5.5 %convert_reduce_fusion.2 = f32[128,1024]{1,0:T(8,128)S(1)} fusion(s32[128,64]{1,0:T(8,128)S(1)} %copy.48), kind=kLoop, calls=%fused_computation.3.clone.1 | loop fusion | flops 25034752 | bytes 557056 | tf_op jit(solution)/shard_map/while/body/eval_jaxpr/reduce_sum | solution.py:48
  280.6 5.5 %convert_reduce_fusion.2 = f32[128,1024]{1,0:T(8,128)S(1)} fusion(s32[128,64]{1,0:T(8,128)S(1)} %copy.48), kind=kLoop, calls=%fused_computation.3.clone.1 | loop fusion | flops 25034752 | bytes 557056 | tf_op jit(solution)/shard_map/while/body/eval_jaxpr/reduce_sum | solution.py:48
  287.5 30.1 %all_to_all.28 = f32[4,1024,128]{2,1,0:T(8,128)} all-to-all(f32[4,1024,128]{2,1,0:T(8,128)} %bitcast.68), channel_id=1, replica_groups=mesh['row'=4,'col'=64] {'row'}, dimensions={0} | all-to-all | bytes 4194304 | tf_op jit(solution)/shard_map/all_to_all | solution.py:36
  320.1 14.7 %all-to-all-start.2 = ((f32[1024,1,128]{2,1,0:T(1,128)}), f32[1024,1,128]{2,1,0:T(1,128)S(1)}, u32[]{:S(2)}, u32[]{:S(2)}) async-start(f32[1024,1,128]{2,1,0:T(1,128)} %bitcast.16), calls=%async_computation.2 | async-start | bytes 1048576 | tf_op jit(solution)/shard_map/all_to_all | solution.py:110
  334.9 17.9 %all-to-all-done.2 = f32[1024,1,128]{2,1,0:T(1,128)S(1)} async-done(((f32[1024,1,128]{2,1,0:T(1,128)}), f32[1024,1,128]{2,1,0:T(1,128)S(1)}, u32[]{:S(2)}, u32[]{:S(2)}) %all-to-all-start.2) | async-done | bytes 524320 | tf_op jit(solution)/shard_map/all_to_all | solution.py:110
  356.7 25.2 %gather_fusion = bf16[2080,16]{1,0:T(8,128)(2,1)} fusion(bf16[16,65,65]{0,2,1:T(8,128)(2,1)S(1)} %copy.41, s32[2080]{0:T(1024)S(1)} %copy-done.1), kind=kCustom, calls=%fused_computation.2 | custom fusion | bytes 149760 | tf_op jit(solution)/shard_map/gather | solution.py:117
  (283 shorter events, 147.1 us)
Async XLA Ops:
  0.6 382.5 %copy-start = (bf16[1024,1024]{1,0:T(8,128)(2,1)S(1)}, bf16[1024,1024]{1,0:T(8,128)(2,1)}, u32[]{:S(2)}) copy-start(bf16[1024,1024]{1,0:T(8,128)(2,1)} %param.24) | copy-start | bytes 6291460
  9.1 6.1 %copy-start.4 = (s32[4096,1]{0,1:T(1,128)S(1)}, s32[4096,1]{0,1:T(1,128)}, u32[]{:S(2)}) copy-start(s32[4096,1]{0,1:T(1,128)} %param.21) | copy-start | bytes 49156
  10.0 12.3 %all-to-all-start = ((f32[4,2,128,128]{3,2,1,0:T(8,128)}), f32[4,2,128,128]{3,2,1,0:T(8,128)S(1)}, u32[]{:S(2)}, u32[]{:S(2)}) async-start(f32[4,2,128,128]{3,2,1,0:T(8,128)} %bitcast.12), calls=%async_computation | async-start | bytes 1048576 | tf_op jit(solution)/shard_map/all_to_all | solution.py:91
  15.2 7.8 %copy-start.3 = (s32[1,8]{1,0:T(1,128)S(1)}, s32[1,8]{1,0:T(1,128)}, u32[]{:S(2)}) copy-start(s32[1,8]{1,0:T(1,128)} %param.19) | copy-start | bytes 100
  287.5 30.1 %copy-start.2 = (f32[1024,128]{1,0:T(8,128)}, f32[1024,128]{1,0:T(8,128)S(1)}, u32[]{:S(2)}) copy-start(f32[1024,128]{1,0:T(8,128)S(1)} %get-tuple-element.156) | copy-start | bytes 1572868
  317.6 17.3 %copy-start.5 = (bf16[16,128]{1,0:T(8,128)(2,1)S(1)}, bf16[16,128]{1,0:T(8,128)(2,1)}, u32[]{:S(2)}) copy-start(bf16[16,128]{1,0:T(8,128)(2,1)} %param.22) | copy-start | bytes 12292
  317.6 17.3 %copy-start.6 = (bf16[1024]{0:T(1024)(128)(2,1)S(1)}, bf16[1024]{0:T(1024)(128)(2,1)}, u32[]{:S(2)}) copy-start(bf16[1024]{0:T(1024)(128)(2,1)} %param.25) | copy-start | bytes 6148
  320.1 36.5 %copy-start.1 = (s32[2080]{0:T(1024)S(1)}, s32[2080]{0:T(1024)}, u32[]{:S(2)}) copy-start(s32[2080]{0:T(1024)} %constant.216) | copy-start | bytes 24964
  320.1 32.7 %all-to-all-start.2 = ((f32[1024,1,128]{2,1,0:T(1,128)}), f32[1024,1,128]{2,1,0:T(1,128)S(1)}, u32[]{:S(2)}, u32[]{:S(2)}) async-start(f32[1024,1,128]{2,1,0:T(1,128)} %bitcast.16), calls=%async_computation.2 | async-start | bytes 1048576 | tf_op jit(solution)/shard_map/all_to_all | solution.py:110
where the time goes:
time: 389 us; the launch traced here: 387 us
  other arithmetic  195 us (50%)
  local copies, waits for them, and re-layouts  66.6 us (17%)
  matrix products  46.2 us (12%)
  blocking collectives  35.2 us (9%)
  waiting for transfers between devices  23.9 us (6%)
  starting transfers between devices  18.2 us (5%)
    reduce_sum x32, other arithmetic, pool_group(): jnp.sum((rows_here[:, :, None] == local_order[None, None, :]).astype(jnp....  177 us
    dot_general x32, matrix products, pool_group(): jnp.dot(counts, table_rows, precision=strict_precision, preferred_element...  40.5 us
    dynamic_slice x32, local copies, waits for them, and re-layouts, pool_range(): lax.map(lambda bag_rows: pool_group(bag_rows, block_ids, table_rows), gro...  31.2 us
    all_to_all x1, blocking collectives, sent_and_summed(): lax.all_to_all(tiles, axis, split_axis=0, concat_axis=0, tiled=True)  30.1 us
    gather x1, local copies, waits for them, and re-layouts, shards(): crossed = interaction_matrix[:, upper_index, lower_index]  25.2 us
    all_to_all x1, waiting for transfers between devices, shards(): lax.all_to_all(summed[:, None, :], 'col', split_axis=0, concat_axis=1, ti...  17.9 us
    all_to_all x1, starting transfers between devices, shards(): lax.all_to_all(summed[:, None, :], 'col', split_axis=0, concat_axis=1, ti...  14.7 us
  transfers between devices with their start and end apart: 2, of which 2 were waited for; matrix products, arithmetic and copies ran while one was open for 1% of the time, Pallas kernels for 0%

commit v1 on v0

v1 whole, which is shorter than its diff:
```python
import functools
import math

import jax
import jax.numpy as jnp
import numpy as np
from jax import lax
from jax.experimental import pallas as pl
from jax.experimental.pallas import tpu as pltpu
from jax.sharding import PartitionSpec as P

BLK = 128
BF16 = jnp.bfloat16
F32 = jnp.float32


def halves(x):
    top = x.astype(BF16)
    rest = (x - top.astype(F32)).astype(BF16)
    return top, rest


def count_kernel(rank_ref, index_ref, length_ref, counts_ref, block_key, offset_key, staged):
    bag = index_ref.shape[0]
    group = index_ref.shape[1]
    half = group // 2
    blocks = counts_ref.shape[0]
    pitch = staged.shape[0] // group
    place = lax.broadcasted_iota(jnp.int32, (bag, group), 0)
    rows = jnp.where(place < length_ref[...], index_ref[...], -1)
    rows = jnp.transpose(rows, (1, 0))
    block = rows // BLK
    block = jnp.where(rows < 0, -1, lax.shift_right_arithmetic(rows, 7))
    offset = rows & (BLK - 1)
    second = jnp.where(block[half:] < 0, -1, block[half:] + blocks)
    block_key[...] = jnp.concatenate([block[:half], second], axis=1)
    offset_key[...] = jnp.concatenate([offset[:half], offset[half:]], axis=1)
    block_order = lax.broadcasted_iota(jnp.int32, (2 * blocks, 2 * bag), 0)
    offset_order = lax.broadcasted_iota(jnp.int32, (BLK, 2 * bag), 0)

    def pair(n):
        in_block = jnp.where(block_key[pl.ds(n, 1), :] == block_order, 1.0, 0.0).astype(BF16)
        at_offset = jnp.where(offset_key[pl.ds(n, 1), :] == offset_order, 1.0, 0.0).astype(BF16)
        found = lax.dot_general(
            in_block, at_offset, (((1,), (1,)), ((), ())), preferred_element_type=F32
        )
        staged[pl.ds(pl.multiple_of(n * pitch, 8), blocks), :] = found[:blocks]
        staged[pl.ds(pl.multiple_of((n + half) * pitch, 8), blocks), :] = found[blocks:]

    def some(step, carry):
        for k in range(8):
            pair(step * 8 + k)
        return carry

    lax.fori_loop(0, half // 8, some, 0)
    for b in range(blocks):
        counts_ref[b] = staged[pl.ds(b, group, stride=pitch), :].astype(BF16)


def count_bags(rank, index, length, share, blocks):
    bag = index.shape[0]
    group = 128
    steps = share // group
    return pl.pallas_call(
        count_kernel,
        grid_spec=pltpu.PrefetchScalarGridSpec(
            num_scalar_prefetch=1,
            grid=(steps,),
            in_specs=[
                pl.BlockSpec((bag, group), lambda g, rank: (0, rank[0] * steps + g)),
                pl.BlockSpec((1, group), lambda g, rank: (0, rank[0] * steps + g)),
            ],
            out_specs=pl.BlockSpec((blocks, group, BLK), lambda g, rank: (0, g, 0)),
            scratch_shapes=[
                pltpu.VMEM((group // 2, 2 * bag), jnp.int32),
                pltpu.VMEM((group // 2, 2 * bag), jnp.int32),
                pltpu.VMEM((group * (blocks + 8), BLK), F32),
            ],
        ),
        out_shape=jax.ShapeDtypeStruct((blocks, share, BLK), BF16),
        name="count_bags",
    )(rank, index, length)


def pool_kernel(
    held_ref, wanted_ref, counts_ref, part0, part1, part2, part3, pooled_ref, moved_ref,
    split_rows, total, target,
):
    step = pl.program_id(0)
    parts = (part0, part1, part2, part3)
    slots = part0.shape[0]
    width = part0.shape[2]

    @pl.when(step == 0)
    def _():
        for b in range(len(parts) * slots):
            target[b] = -1
        for s in range(slots):
            target[wanted_ref[s]] = s
        for k, part in enumerate(parts):
            for s in range(slots):
                b = held_ref[k * slots + s]
                rows = part[s]
                top, rest = halves(rows)
                split_rows[b, :, :width] = top
                split_rows[b, :, width:] = rest
                goal = target[b]

                @pl.when(goal >= 0)
                def _(part=part, s=s, goal=goal):
                    moved_ref[goal] = part[s]

    pair = counts_ref.shape[0]
    left = jnp.concatenate([counts_ref[k] for k in range(pair)], axis=1)
    right = split_rows[pl.ds(step * pair, pair)].reshape(pair * BLK, 2 * width)
    found = lax.dot_general(left, right, (((1,), (0,)), ((), ())), preferred_element_type=F32)

    @pl.when(step == 0)
    def _():
        total[...] = found

    @pl.when(step > 0)
    def _():
        total[...] += found

    @pl.when(step == pl.num_programs(0) - 1)
    def _():
        pooled_ref[...] = total[:, :width] + total[:, width:]


def pool_and_move(held, wanted, counts, parts):
    blocks, share, _ = counts.shape
    slots, _, width = parts[0].shape
    pair = 2
    whole = pl.BlockSpec((slots, BLK, width), lambda j, *_: (0, 0, 0))
    return pl.pallas_call(
        pool_kernel,
        grid_spec=pltpu.PrefetchScalarGridSpec(
            num_scalar_prefetch=2,
            grid=(blocks // pair,),
            in_specs=[pl.BlockSpec((pair, share, BLK), lambda j, *_: (j, 0, 0))] + [whole] * 4,
            out_specs=[
                pl.BlockSpec((share, width), lambda j, *_: (0, 0)),
                whole,
            ],
            scratch_shapes=[
                pltpu.VMEM((blocks, BLK, 2 * width), BF16),
                pltpu.VMEM((share, 2 * width), F32),
                pltpu.SMEM((blocks,), jnp.int32),
            ],
        ),
        out_shape=[
            jax.ShapeDtypeStruct((share, width), F32),
            jax.ShapeDtypeStruct((slots, BLK, width), F32),
        ],
        name="pool_and_move",
    )(held, wanted, counts, *parts)


def top_kernel(
    pooled_ref, dense_ref, first_hbm, second_hbm, out_ref, logits_ref,
    first, second, gram, joined, sems,
):
    samples, width = dense_ref.shape
    tables = pooled_ref.shape[0] // samples
    pitch = gram.shape[0] // samples
    inputs = first_hbm.shape[0]
    fetch_first = pltpu.make_async_copy(first_hbm, first.at[pl.ds(0, inputs)], sems.at[0])
    fetch_second = pltpu.make_async_copy(second_hbm, second, sems.at[1])
    fetch_first.start()
    fetch_second.start()
    first[inputs:, :] = jnp.zeros((first.shape[0] - inputs, first.shape[1]), BF16)
    dense = dense_ref[...].astype(F32)
    for s in range(samples):
        top, rest = halves(pooled_ref[pl.ds(s, tables, stride=samples), :])
        own = jnp.broadcast_to(dense[s : s + 1], (8, width)).astype(BF16)
        none = jnp.zeros((8, width), BF16)
        tall_top = jnp.concatenate([top, own], axis=0)
        tall_rest = jnp.concatenate([rest, none], axis=0)
        left = jnp.concatenate([tall_top, tall_rest, tall_top], axis=1)
        right = jnp.concatenate([top, top, rest], axis=1)
        found = lax.dot_general(
            left, right, (((1,), (1,)), ((), ())), preferred_element_type=F32
        )
        gram[s * pitch : (s + 1) * pitch, :tables] = found * width ** (-0.5)
    lane = lax.broadcasted_iota(jnp.int32, (samples, 128), 1)
    joined[:, :width] = dense_ref[...]
    at = width
    filling = jnp.zeros((samples, 128), F32)
    for i in range(-1, tables - 1):
        row = tables if i < 0 else i
        start = 0 if i < 0 else i + 1
        line = gram[pl.ds(row, samples, stride=pitch), :]
        shift = (at - start) % 128
        line = pltpu.roll(line, shift, 1) if shift else line
        filling = jnp.where(lane >= at % 128, line, filling)
        after = at + tables - start
        if after // 128 != at // 128:
            base = at // 128 * 128
            joined[:, base : base + 128] = filling.astype(BF16)
            filling = line
        at = after
    base = at // 128 * 128
    if at % 128:
        joined[:, base : base + 128] = jnp.where(lane < at % 128, filling, 0.0).astype(BF16)
    fetch_first.wait()
    hidden = jnp.dot(joined[...], first[...], preferred_element_type=F32)
    hidden = jnp.maximum(hidden, 0.0).astype(BF16)
    fetch_second.wait()
    hidden = jnp.dot(hidden, second[...], preferred_element_type=F32)
    hidden = jnp.maximum(hidden, 0.0).astype(BF16)
    last = jnp.broadcast_to(out_ref[...], (16, hidden.shape[1]))
    answer = lax.dot_general(last, hidden, (((1,), (1,)), ((), ())), preferred_element_type=F32)
    logits_ref[...] = answer[:1]


def top_of_model(pooled, dense, w_first, w_second, w_out):
    samples, width = dense.shape
    tables = pooled.shape[0] // samples
    inputs, hidden = w_first.shape
    padded = -(-inputs // 128) * 128
    vmem = pl.BlockSpec(memory_space=pltpu.VMEM)
    hbm = pl.BlockSpec(memory_space=pl.ANY)
    return pl.pallas_call(
        top_kernel,
        in_specs=[vmem, vmem, hbm, hbm, vmem],
        out_specs=vmem,
        out_shape=jax.ShapeDtypeStruct((1, samples), F32),
        scratch_shapes=[
            pltpu.VMEM((padded, hidden), BF16),
            pltpu.VMEM(w_second.shape, BF16),
            pltpu.VMEM((samples * (tables + 8), 128), F32),
            pltpu.VMEM((samples, padded), BF16),
            pltpu.SemaphoreType.DMA((2,)),
        ],
        name="top_of_model",
    )(pooled, dense, w_first, w_second, w_out.reshape(1, -1))


def shards(
    old_table, old_blocks, new_blocks, bag_row_index, bag_length, dense, w_first, w_second, w_out
):
    slots = old_blocks.shape[1]
    width = old_table.shape[2]
    rows = lax.axis_size("row")
    rank = lax.axis_index("row")
    own = old_table[0].reshape(slots, BLK, width)
    other_core = [(k, k ^ 1) for k in range(rows)]
    other_chip = [(k, k ^ 2) for k in range(rows)]
    both = [(k, k ^ 3) for k in range(rows)]
    ids = old_blocks[0]
    across = lax.ppermute(own, "row", other_chip)
    beside = lax.ppermute(own, "row", other_core)
    far = lax.ppermute(across, "row", other_core)
    held = jnp.concatenate(
        [
            ids,
            lax.ppermute(ids, "row", other_core),
            lax.ppermute(ids, "row", other_chip),
            lax.ppermute(ids, "row", both),
        ]
    )
    share = bag_row_index.shape[0] // rows
    counts = count_bags(
        rank.astype(jnp.int32)[None],
        jnp.transpose(bag_row_index[:, 0, :]),
        jnp.transpose(bag_length),
        share,
        rows * slots,
    )
    pooled, moved = pool_and_move(held, new_blocks[0], counts, (own, beside, across, far))
    cols = lax.axis_size("col")
    spread = lax.all_to_all(
        pooled.reshape(cols, share // cols, width), "col", split_axis=0, concat_axis=0, tiled=True
    )
    logits = top_of_model(spread.reshape(share, width), dense, w_first, w_second, w_out)
    return logits.reshape(-1), moved.reshape(1, slots * BLK, width)


def solution(mesh):
    in_specs = (
        P("col", "row", None),
        P("col", "row"),
        P("col", "row"),
        P(None, "col", None),
        P(None, "col"),
        P(("row", "col"), None),
        P(),
        P(),
        P(),
    )
    out_specs = (P(("row", "col")), P("col", "row", None))
    return jax.shard_map(shards, mesh=mesh, in_specs=in_specs, out_specs=out_specs, check_vma=False)
```

time: 389 us -> 99.5 us (0.26)
  other arithmetic: 195 us -> 0.59 us
  local copies, waits for them, and re-layouts: 66.6 us -> 2.4 us
  matrix products: 46.2 us -> 0 us
  Pallas kernels: 0 us -> 45.3 us
  blocking collectives: 35.2 us -> 0 us
  waiting for transfers between devices: 23.9 us -> 31.1 us
    reduce_sum x68 -> x0, other arithmetic: 185 us -> none  [the longest x32 177 us: pool_group(): jnp.sum((rows_here[:, :, None] == local_order[None, None, :]).astype(jnp....]
    dot_general x35 -> x0, matrix products: 46.2 us -> none  [the longest x32 40.5 us: pool_group(): jnp.dot(counts, table_rows, precision=strict_precision, preferred_element...]
    pallas_call x0 -> x3, Pallas kernels: none -> 45.3 us  [the longest x1 24.3 us: count_bags(): pl.pallas_call(count_kernel, grid_spec=pltpu.PrefetchScalarGridSpec(num_s...]
    dynamic_slice x32 -> x0, local copies, waits for them, and re-layouts: 31.2 us -> none  [pool_range(): lax.map(lambda bag_rows: pool_group(bag_rows, block_ids, table_rows), gro...]
    all_to_all x1 -> x0, blocking collectives: 30.1 us -> none  [sent_and_summed(): lax.all_to_all(tiles, axis, split_axis=0, concat_axis=0, tiled=True)]
    gather x3 -> x0, local copies, waits for them, and re-layouts: 27.4 us -> none  [the longest x1 25.2 us: shards(): crossed = interaction_matrix[:, upper_index, lower_index]]
    ppermute x0 -> x6, waiting for transfers between devices: none -> 12.4 us  [the longest x1 12.4 us: shards(): across = lax.ppermute(own, 'row', other_chip)]
    all_to_all x2 -> x1, waiting for transfers between devices: 23.9 us -> 18.7 us  [shards(): lax.all_to_all(pooled.reshape(cols, share // cols, width), 'col', split_a...]
  transfers between devices with their start and end apart: 2 -> 7, of which waited for: 2 -> 2; matrix products, arithmetic and copies ran while one was open for 1% -> 1% of each run, Pallas kernels for 0% -> 25%
where the time goes in v1:
time: 99.5 us; the launch traced here: 98 us
  Pallas kernels  45.3 us (46%)
  waiting for transfers between devices  31.1 us (31%)
  starting transfers between devices  18 us (18%)
  local copies, waits for them, and re-layouts  2.4 us (2%)
    pallas_call x1, Pallas kernels, count_bags(): pl.pallas_call(count_kernel, grid_spec=pltpu.PrefetchScalarGridSpec(num_s...  24.3 us
    all_to_all x1, waiting for transfers between devices, shards(): lax.all_to_all(pooled.reshape(cols, share // cols, width), 'col', split_a...  18.7 us
    pallas_call x1, Pallas kernels, pool_and_move(): pl.pallas_call(pool_kernel, grid_spec=pltpu.PrefetchScalarGridSpec(num_sc...  15.3 us
    all_to_all x1, starting transfers between devices, shards(): lax.all_to_all(pooled.reshape(cols, share // cols, width), 'col', split_a...  14.4 us
    ppermute x1, waiting for transfers between devices, shards(): across = lax.ppermute(own, 'row', other_chip)  12.4 us
    pallas_call x1, Pallas kernels, top_of_model(): pl.pallas_call(top_kernel, in_specs=[vmem, vmem, hbm, hbm, vmem], out_spe...  5.67 us
  transfers between devices with their start and end apart: 7, of which 2 were waited for; matrix products, arithmetic and copies ran while one was open for 1% of the time, Pallas kernels for 25%

profile of v1, /device:TPU:8, one launch (start us, length us, event | category | flops | bytes accessed | tf_op | source)
XLA Modules:
  0.0 98.0 jit_solution(12118284178361858691)
XLA Ops:
  0.6 1.6 %collective-permute-start.4 = (f32[8,128,128]{2,1,0:T(8,128)}, f32[8,128,128]{2,1,0:T(8,128)S(1)}, u32[]{:S(2)}, u32[]{:S(2)}) collective-permute-start(f32[8,128,128]{2,1,0:T(8,128)} %bitcast.15), channel_id=1, source_target_pairs={{0,128},{64,192},{128,0},{192,64},{1,129},{65,193},{129,1},{193,65... | collective-permute-start | bytes 1572872 | tf_op jit(solution)/shard_map/ppermute | solution.py:252
  2.2 0.0 collective-permute-start.3
  2.2 12.4 %collective-permute-done.4.part2 = f32[8,128,128]{2,1,0:T(8,128)S(1)} collective-permute-done((f32[8,128,128]{2,1,0:T(8,128)}, f32[8,128,128]{2,1,0:T(8,128)S(1)}, u32[]{:S(2)}, u32[]{:S(2)}) %collective-permute-start.4) | collective-permute-done | bytes 524320 | tf_op jit(solution)/shard_map/ppermute | solution.py:252
  14.6 0.0 copy-start.1
  14.6 0.0 collective-permute-start.5
  14.6 0.5 collective-permute-start
  15.1 1.5 %collective-permute-start.1 = (s32[8]{0:T(128)}, s32[8]{0:T(128)S(1)}, u32[]{:S(2)}, u32[]{:S(2)}) collective-permute-start(s32[8]{0:T(128)} %bitcast.22), channel_id=1, source_target_pairs={{0,128},{64,192},{128,0},{192,64},{1,129},{65,193},{129,1},{193,65... | collective-permute-start | bytes 104 | tf_op jit(solution)/shard_map/ppermute | solution.py:259
  16.6 0.0 collective-permute-start.2
  16.6 0.0 copy-start.5
  16.6 24.3 %count_bags.1.counts_ref = bf16[32,1024,128]{2,1,0:T(8,128)(2,1)} custom-call(s32[1]{0:T(128)} %bitcast.2.rank_ref, s32[64,4096]{1,0:T(8,128)} %bitcast.13, s32[1,4096]{1,0:T(1,128)} %bitcast.18), custom_call_target="tpu_custom_call" | custom-call | tf_op jit(solution)/shard_map/count_bags/pallas_call | solution.py:64
  40.9 0.0 copy-done.1
  40.9 0.0 collective-permute-done
  40.9 0.0 collective-permute-done.1
  40.9 0.0 collective-permute-done.2
  40.9 0.0 copy-done.5
  40.9 0.6 pad_add_fusion.held_ref
  41.5 0.0 collective-permute-done.3.part1
  41.5 0.0 copy-start.2
  41.5 0.0 collective-permute-done.5.part3
  41.5 0.0 copy-start.3
  41.5 0.8 copy-done.2
  42.4 0.2 copy-done.3
  42.5 0.0 copy-start.4
  42.5 15.3 %pool_and_move.1 = (f32[1024,128]{1,0:T(8,128)}, f32[8,128,128]{2,1,0:T(8,128)}) custom-call(s32[32]{0:T(128)} %pad_add_fusion.held_ref, s32[8]{0:T(128)} %bitcast.19, bf16[32,1024,128]{2,1,0:T(8,128)(2,1)} %count_bags.1.counts_ref, f32[8,128,128]{2,1,0:T(8,128)} %bitcast.17, f32[8,128,128]{2,1,0:T(8,128)} %copy-done.2, f32[8,128,128]{2,1,0:T(8,128)} %copy-done.1, ...), custom_call_target="tpu_custom_call" | custom-call | tf_op jit(solution)/shard_map/pool_and_move/pallas_call | solution.py:136
  57.8 14.4 %all-to-all-start = ((f32[64,16,128]{2,1,0:T(8,128)}), f32[64,16,128]{2,1,0:T(8,128)S(1)}, u32[]{:S(2)}, u32[]{:S(2)}) async-start(f32[64,16,128]{2,1,0:T(8,128)} %bitcast.14), calls=%async_computation | async-start | bytes 1048576 | tf_op jit(solution)/shard_map/all_to_all | solution.py:273
  72.3 0.0 copy-done.4
  72.3 0.6 reshape.21.out_ref
  72.9 18.7 %all-to-all-done = f32[64,16,128]{2,1,0:T(8,128)S(1)} async-done(((f32[64,16,128]{2,1,0:T(8,128)}), f32[64,16,128]{2,1,0:T(8,128)S(1)}, u32[]{:S(2)}, u32[]{:S(2)}) %all-to-all-start) | async-done | bytes 524320 | tf_op jit(solution)/shard_map/all_to_all | solution.py:273
  91.5 0.0 copy-start
  91.5 0.8 copy-done
  92.3 5.7 %top_of_model.1 = f32[1,16]{1,0:T(1,128)} custom-call(f32[1024,128]{1,0:T(8,128)} %bitcast.12, bf16[16,128]{1,0:T(8,128)(2,1)} %dense_ref.1, bf16[2208,1024]{1,0:T(8,128)(2,1)} %first_hbm.1, bf16[1024,1024]{1,0:T(8,128)(2,1)} %second_hbm.1, bf16[1,1024]{1,0:T(2,128)(2,1)} %reshape.21.out_ref), custom_call_target="tpu_custom_call" | custom-call | tf_op jit(solution)/shard_map/top_of_model/pallas_call | solution.py:224
Async XLA Ops:
  0.6 14.0 %collective-permute-start.4 = (f32[8,128,128]{2,1,0:T(8,128)}, f32[8,128,128]{2,1,0:T(8,128)S(1)}, u32[]{:S(2)}, u32[]{:S(2)}) collective-permute-start(f32[8,128,128]{2,1,0:T(8,128)} %bitcast.15), channel_id=1, source_target_pairs={{0,128},{64,192},{128,0},{192,64},{1,129},{65,193},{129,1},{193,65... | collective-permute-start | bytes 1572872 | tf_op jit(solution)/shard_map/ppermute | solution.py:252
  2.2 39.3 %collective-permute-start.3 = (f32[8,128,128]{2,1,0:T(8,128)}, f32[8,128,128]{2,1,0:T(8,128)S(1)}, u32[]{:S(2)}, u32[]{:S(2)}) collective-permute-start(f32[8,128,128]{2,1,0:T(8,128)} %bitcast.16), channel_id=1, source_target_pairs={{0,64},{64,0},{128,192},{192,128},{1,65},{65,1},{129,193},{193,129... | collective-permute-start | bytes 1572872 | tf_op jit(solution)/shard_map/ppermute | solution.py:253
  14.6 26.3 %copy-start.1 = (f32[8,128,128]{2,1,0:T(8,128)}, f32[8,128,128]{2,1,0:T(8,128)S(1)}, u32[]{:S(2)}) copy-start(f32[8,128,128]{2,1,0:T(8,128)S(1)} %collective-permute-done.4.part2) | copy-start | bytes 1572868
  14.6 26.9 %collective-permute-start.5 = (f32[8,128,128]{2,1,0:T(8,128)S(1)}, f32[8,128,128]{2,1,0:T(8,128)S(1)}, u32[]{:S(2)}, u32[]{:S(2)}) collective-permute-start(f32[8,128,128]{2,1,0:T(8,128)S(1)} %collective-permute-done.4.part2), channel_id=1, source_target_pairs={{0,64},{64,0},{128,192},{192,128},{1,65},{65,1},{129,193},{193,129... | collective-permute-start | bytes 1572872 | tf_op jit(solution)/shard_map/ppermute | solution.py:254
  14.6 26.3 %collective-permute-start = (s32[8]{0:T(128)}, s32[8]{0:T(128)S(1)}, u32[]{:S(2)}, u32[]{:S(2)}) collective-permute-start(s32[8]{0:T(128)} %bitcast.21), channel_id=1, source_target_pairs={{0,64},{64,0},{128,192},{192,128},{1,65},{65,1},{129,193},{193,129... | collective-permute-start | bytes 104 | tf_op jit(solution)/shard_map/ppermute | solution.py:258
  15.1 25.8 %collective-permute-start.1 = (s32[8]{0:T(128)}, s32[8]{0:T(128)S(1)}, u32[]{:S(2)}, u32[]{:S(2)}) collective-permute-start(s32[8]{0:T(128)} %bitcast.22), channel_id=1, source_target_pairs={{0,128},{64,192},{128,0},{192,64},{1,129},{65,193},{129,1},{193,65... | collective-permute-start | bytes 104 | tf_op jit(solution)/shard_map/ppermute | solution.py:259
  16.6 24.3 %collective-permute-start.2 = (s32[8]{0:T(128)}, s32[8]{0:T(128)S(1)}, u32[]{:S(2)}, u32[]{:S(2)}) collective-permute-start(s32[8]{0:T(128)} %bitcast.23), channel_id=1, source_target_pairs={{0,192},{64,128},{128,64},{192,0},{1,193},{65,129},{129,65},{193,1... | collective-permute-start | bytes 104 | tf_op jit(solution)/shard_map/ppermute | solution.py:260
  16.6 24.3 %copy-start.5 = (s32[1,8]{1,0:T(1,128)S(1)}, s32[1,8]{1,0:T(1,128)}, u32[]{:S(2)}) copy-start(s32[1,8]{1,0:T(1,128)} %param.10) | copy-start | bytes 100
  41.5 0.8 copy-start.2
  41.5 1.0 %copy-start.3 = (f32[8,128,128]{2,1,0:T(8,128)}, f32[8,128,128]{2,1,0:T(8,128)S(1)}, u32[]{:S(2)}) copy-start(f32[8,128,128]{2,1,0:T(8,128)S(1)} %collective-permute-done.5.part3) | copy-start | bytes 1572868
  42.5 29.7 %copy-start.4 = (bf16[1024]{0:T(1024)(128)(2,1)S(1)}, bf16[1024]{0:T(1024)(128)(2,1)}, u32[]{:S(2)}) copy-start(bf16[1024]{0:T(1024)(128)(2,1)} %param.17) | copy-start | bytes 6148
  57.8 33.7 %all-to-all-start = ((f32[64,16,128]{2,1,0:T(8,128)}), f32[64,16,128]{2,1,0:T(8,128)S(1)}, u32[]{:S(2)}, u32[]{:S(2)}) async-start(f32[64,16,128]{2,1,0:T(8,128)} %bitcast.14), calls=%async_computation | async-start | bytes 1048576 | tf_op jit(solution)/shard_map/all_to_all | solution.py:273
  91.5 0.8 copy-start
